TPU v7x, 32 devices: a whole 2x2x4 slice. The times are simulated.
32 devices in a mesh: farcp: 4 (over x, core), nearcp: 2 (over y), heads: 4 (over z).
Axes of the slice: x: 2, y: 2, z: 4, core: 2. Of those that a mesh axis runs over, the one named last changes fastest.
Arguments:
- raw_keys: bfloat16 [8, 2048, 8, 128], P(None, ('farcp', 'nearcp'), 'heads'), may hold values from -6 to 6
- raw_values: bfloat16 [8, 2048, 8, 128], P(None, ('farcp', 'nearcp'), 'heads'), may hold values from -6 to 6
- turn_angle: float32 [2048, 64], replicated, may hold values from -3.140625 to 3.140625
- key_gain: float32 [128], replicated, may hold values from 0.25 to 1.75
Outputs:
- cache_keys: bfloat16 [8, 2048, 8, 128], P(('farcp', 'nearcp'), None, 'heads')
- cache_values: bfloat16 [8, 2048, 8, 128], P(('farcp', 'nearcp'), None, 'heads')
- key_scale: float32 [8, 8, 128], P(('farcp', 'nearcp'), 'heads')
All inputs are finite; a program needn't handle non-finite values. Where the computation divides by a largest or mean magnitude, that divisor is 1e-20 or more.
Results may differ from a plain program's by a relative error of at most 0.001.
Values may be sent and summed in bfloat16 or wider, within the bound.
A program may use at most 128 MiB of HBM per device.

v0:
```python
import functools

import jax
import jax.numpy as jnp
from jax import lax
from jax.experimental import pallas as pl
from jax.experimental.pallas import tpu as pltpu
from jax.sharding import PartitionSpec as P

MESH = pl.DeviceIdType.MESH
LANES = 128
SUBLANES = 8
BLOCK = 128
SINE = (1.0, -0.1666666716337204, 0.008333330973982811, -0.00019840861205011606,
        2.752528644123231e-06, -2.3889498379503493e-08)
COSINE = (1.0, -0.5, 0.0416666679084301, -0.0013888884568586946, 2.4801040126476437e-05,
          -2.752468617472914e-07, 1.9907717696554528e-09)


def polynomial(coefficients, z):
    total = jnp.full_like(z, coefficients[-1])
    for coefficient in coefficients[-2::-1]:
        total = total * z + coefficient
    return total


def cosine_and_sine(angle):
    y = (1.57079637 - jnp.abs(angle)) - 4.371139e-08
    z = y * y
    sine = polynomial(COSINE, z)
    return y * polynomial(SINE, z), jnp.where(angle < 0, -sine, sine)


def partner(index, offset, size):
    result, bit = 0, 1
    while bit < size:
        digit = (index // bit) % 2
        result = result + ((digit + 1) % 2 if offset & bit else digit) * bit
        bit *= 2
    return result


def place_of(device):
    return {"farcp": device[0], "nearcp": device[1]}


def kernel(far, near, heads, offsets, keys, values, angle, gain, out_keys, out_values, out_scale,
           landed, held_keys, turned, cosines, sines, angles, gains, send_sem, recv_sem, local_sem, ready):
    members, rows, _ = landed.shape
    far_index, near_index = lax.axis_index("farcp"), lax.axis_index("nearcp")
    me = far_index * near + near_index
    one_link = [o for o in offsets if o[0] < 2 or o[1] == 0]
    two_links = [o for o in offsets if o not in one_link]
    peers = [
        (partner(far_index, f, far), partner(near_index, n, near)) for f, n in offsets
    ]

    def own(i, source, target):
        return pltpu.make_async_copy(source, target, local_sem.at[i])

    local = [
        own(0, angle, angles),
        own(1, gain, gains),
        own(2, keys, held_keys),
        own(3, values.at[me], out_values.at[me]),
    ]
    local[2].start()

    barrier = pltpu.get_barrier_semaphore()
    beside = [device for device, offset in zip(peers, offsets) if offset in one_link]
    for device in beside:
        pl.semaphore_signal(barrier, inc=1, device_id=place_of(device), device_id_type=MESH)
    local[2].wait()
    pl.semaphore_wait(barrier, len(beside))
    same_far = [device for device, (f, n) in zip(peers, offsets) if f == 0]
    for device in same_far:
        pl.semaphore_signal(ready, inc=1, device_id=place_of(device), device_id_type=MESH)

    sends = {}
    for i, (source, target) in enumerate(((held_keys, landed), (values, out_values))):
        for offset, (f, n) in zip(offsets, peers):
            sends[i, offset] = pltpu.make_async_remote_copy(
                src_ref=source.at[f * near + n],
                dst_ref=target.at[me],
                send_sem=send_sem.at[i, offsets.index(offset)],
                recv_sem=recv_sem.at[i, offsets.index(offset)],
                device_id=place_of((f, n)),
                device_id_type=MESH,
            )
    for i, batch in ((0, one_link), (0, two_links), (1, two_links), (1, one_link)):
        if (i, batch) == (0, two_links):
            pl.semaphore_wait(ready, len(same_far))
        for offset in batch:
            sends[i, offset].start()

    for copy in (local[0], local[1], local[3]):
        copy.start()
    local[0].wait()
    local[1].wait()

    @pl.loop(0, angles.shape[1] // LANES)
    def _(step):
        start = pl.multiple_of(step * LANES, LANES)
        cosine, sine = cosine_and_sine(angles[:, pl.ds(start, LANES)])
        gain_row = gains[...]
        turn_same = jnp.concatenate([cosine, cosine], axis=0).T * gain_row
        turn_other = jnp.concatenate([-sine, sine], axis=0).T * pltpu.roll(
            gain_row, LANES // 2, 1
        )
        for head in range(heads):
            place = pl.ds(start * heads + head, LANES, stride=heads)
            cosines[place, :] = turn_same
            sines[place, :] = turn_other

    def turn_block(blocks, slot, largest):
        @functools.partial(lax.fori_loop, 0, rows // BLOCK, init_val=largest)
        def result(step, most):
            start = pl.multiple_of(step * BLOCK, BLOCK)
            place = pl.ds(pl.multiple_of(slot * rows + start, BLOCK), BLOCK)
            x = blocks[slot, pl.ds(start, BLOCK), :].astype(jnp.float32)
            mean = jnp.sum(x * x, axis=-1, keepdims=True) * (1.0 / LANES)
            scaled = x * cosines[place, :] + pltpu.roll(x, LANES // 2, 1) * sines[place, :]
            scaled = scaled * lax.rsqrt(mean + 1e-06)
            turned[place, :] = scaled
            return jnp.maximum(
                most, jnp.max(jnp.abs(scaled).reshape(-1, SUBLANES, LANES), axis=0)
            )

        return result

    most = jnp.zeros((SUBLANES, LANES), jnp.float32)
    most = turn_block(held_keys, me, most)
    for offset in one_link + two_links:
        f, n = peers[offsets.index(offset)]
        sends[0, offset].wait_recv()
        most = turn_block(landed, f * near + n, most)
    scale = most[:heads]
    for row in range(heads, SUBLANES, heads):
        scale = jnp.maximum(scale, most[row : row + heads])
    out_scale[...] = scale
    inverse = jnp.concatenate([1.0 / scale] * (SUBLANES // heads), axis=0)[None]

    @pl.loop(0, members * rows // BLOCK)
    def _(step):
        place = pl.ds(pl.multiple_of(step * BLOCK, BLOCK), BLOCK)
        wide = turned[place, :].reshape(-1, SUBLANES, LANES) * inverse
        out_keys[place, :] = wide.reshape(BLOCK, LANES).astype(out_keys.dtype)

    local[3].wait()
    for offset in offsets:
        sends[1, offset].wait_recv()
    for send in sends.values():
        send.wait_send()


def hold(x):
    return pltpu.with_memory_space_constraint(x, pltpu.HBM)


def write_out(*refs):
    count = len(refs) // 2
    sources, targets, sems = refs[:count], refs[count : 2 * count], refs[-1]
    copies = [
        pltpu.make_async_copy(source, target, sems.at[i])
        for i, (source, target) in enumerate(zip(sources, targets))
    ]
    for copy in copies:
        copy.start()
    for copy in copies:
        copy.wait()


def shards(far, near, raw_keys, raw_values, turn_angle, key_gain):
    batch, length, heads, size = raw_keys.shape
    members = far * near
    assert batch == members and size == LANES and SUBLANES % heads == 0
    assert far & (far - 1) == 0 and near & (near - 1) == 0
    rows = length * heads
    offsets = [(f, n) for f in range(far) for n in range(near) if (f, n) != (0, 0)]
    offsets.sort(key=lambda o: (o[0] < 2 and o[1] == 0, o[1], o[0]))
    anywhere = pl.BlockSpec(memory_space=pl.ANY)
    inside = pl.BlockSpec(memory_space=pltpu.VMEM)
    results = pl.pallas_call(
        functools.partial(kernel, far, near, heads, offsets),
        out_shape=(
            pltpu.VMEM((members * rows, size), raw_keys.dtype),
            pltpu.VMEM((members, rows, size), raw_values.dtype),
            jax.ShapeDtypeStruct((heads, size), jnp.float32),
        ),
        in_specs=[anywhere] * 4,
        out_specs=(inside, inside, inside),
        scratch_shapes=[
            pltpu.VMEM((members, rows, size), raw_keys.dtype),
            pltpu.VMEM((members, rows, size), raw_keys.dtype),
            pltpu.VMEM((members * rows, size), jnp.float32),
            pltpu.VMEM((members * rows, size), jnp.float32),
            pltpu.VMEM((members * rows, size), jnp.float32),
            pltpu.VMEM((size // 2, members * length), jnp.float32),
            pltpu.VMEM((1, size), jnp.float32),
            pltpu.SemaphoreType.DMA((2, len(offsets))),
            pltpu.SemaphoreType.DMA((2, len(offsets))),
            pltpu.SemaphoreType.DMA((4,)),
            pltpu.SemaphoreType.REGULAR,
        ],
        compiler_params=pltpu.CompilerParams(
            collective_id=0, has_side_effects=True, vmem_limit_bytes=32 * 1024 * 1024
        ),
        name="move_and_turn",
    )(
        hold(raw_keys.reshape(batch, rows, size)),
        hold(raw_values.reshape(batch, rows, size)),
        hold(turn_angle.T),
        hold(key_gain.reshape(1, size)),
    )
    narrow_keys, moved_values, key_scale = pl.pallas_call(
        write_out,
        out_shape=tuple(pltpu.HBM(r.shape, r.dtype) for r in results),
        in_specs=[anywhere] * len(results),
        out_specs=(anywhere,) * len(results),
        scratch_shapes=[pltpu.SemaphoreType.DMA((len(results),))],
        compiler_params=pltpu.CompilerParams(vmem_limit_bytes=2 * 1024 * 1024),
        name="write_out",
    )(*results)
    whole = (1, members * length, heads, size)
    return narrow_keys.reshape(whole), moved_values.reshape(whole), key_scale[None]


def solution(mesh):
    in_specs = (
        P(None, ("farcp", "nearcp"), "heads", None),
        P(None, ("farcp", "nearcp"), "heads", None),
        P(),
        P(),
    )
    out_specs = (
        P(("farcp", "nearcp"), None, "heads", None),
        P(("farcp", "nearcp"), None, "heads", None),
        P(("farcp", "nearcp"), "heads", None),
    )
    body = functools.partial(shards, mesh.shape["farcp"], mesh.shape["nearcp"])
    return jax.shard_map(body, mesh=mesh, in_specs=in_specs, out_specs=out_specs, check_vma=False)
```

profile of v0, /device:TPU:0, one launch (start us, length us, event | category | flops | bytes accessed | tf_op | source)
XLA Modules:
  0.0 29.8 jit_solution(15294357255004304852)
XLA Ops:
  0.6 27.8 %move_and_turn.1 = (bf16[4096,128]{1,0:T(8,128)(2,1)S(1)}, bf16[8,512,128]{2,1,0:T(8,128)(2,1)S(1)}, f32[2,128]{1,0:T(2,128)S(1)}) custom-call(bf16[8,512,128]{2,1,0:T(8,128)(2,1)} %bitcast.7, bf16[8,512,128]{2,1,0:T(8,128)(2,1)} %bitcast.8, f32[64,2048]{1,0:T(8,128)} %bitcast.9, f32[1,128]{1,0:T(1,128)} %bitcast.10), custom_call_target="tpu_custom_call" | custom-call | tf_op jit(solution)/shard_map/move_and_turn/pallas_call | solution.py:183
  28.4 1.3 %write_out.1 = (bf16[4096,128]{1,0:T(8,128)(2,1)}, bf16[8,512,128]{2,1,0:T(8,128)(2,1)}, f32[2,128]{1,0:T(2,128)}) custom-call(bf16[4096,128]{1,0:T(8,128)(2,1)S(1)} %get-tuple-element.9.refs_0_, bf16[8,512,128]{2,1,0:T(8,128)(2,1)S(1)} %get-tuple-element.10.refs_1_, f32[2,128]{1,0:T(2,128)S(1)} %get-tuple-element.11.refs_2_), custom_call_target="tpu_custom_call" | custom-call | tf_op jit(solution)/shard_map/write_out/pallas_call | solution.py:215
where the time goes:
time: 30 us; the launch traced here: 29.8 us
  Pallas kernels  29.1 us (97%)
  between operations  0.64 us (2%)
    pallas_call x1, Pallas kernels, shards(): pl.pallas_call(functools.partial(kernel, far, near, heads, offsets), out_...  27.8 us
    pallas_call x1, Pallas kernels, shards(): pl.pallas_call(write_out, out_shape=tuple((pltpu.HBM(r.shape, r.dtype) fo...  1.35 us

commit v1 on v0

--- a/solution.py
+++ b/solution.py
@@ -11,6 +11,7 @@
 LANES = 128
 SUBLANES = 8
 BLOCK = 128
+ROOT, SIDE, END = 0, 1, 2
 SINE = (1.0, -0.1666666716337204, 0.008333330973982811, -0.00019840861205011606,
         2.752528644123231e-06, -2.3889498379503493e-08)
 COSINE = (1.0, -0.5, 0.0416666679084301, -0.0013888884568586946, 2.4801040126476437e-05,
@@ -40,6 +41,10 @@
     return result
 
 
+def role_of(far_index, near_index):
+    return jnp.where(far_index < 2, 0, 1) + jnp.where(near_index == 0, 0, 1)
+
+
 def place_of(device):
     return {"farcp": device[0], "nearcp": device[1]}
 
@@ -51,9 +56,11 @@
     me = far_index * near + near_index
     one_link = [o for o in offsets if o[0] < 2 or o[1] == 0]
     two_links = [o for o in offsets if o not in one_link]
-    peers = [
-        (partner(far_index, f, far), partner(near_index, n, near)) for f, n in offsets
-    ]
+    peers = {
+        (f, n): (partner(far_index, f, far), partner(near_index, n, near)) for f, n in offsets
+    }
+    role, roles = role_of(far_index, near_index), {o: role_of(*peers[o]) for o in offsets}
+    roots, sides, ends = 2, 2 * (near - 1) + far - 2, (far - 2) * (near - 1)
 
     def own(i, source, target):
         return pltpu.make_async_copy(source, target, local_sem.at[i])
@@ -61,24 +68,35 @@
     local = [
         own(0, angle, angles),
         own(1, gain, gains),
-        own(2, keys, held_keys),
+        own(2, keys.at[me], held_keys.at[me]),
         own(3, values.at[me], out_values.at[me]),
     ]
+    loads = {}
+    for i, offset in enumerate(one_link + two_links):
+        f, n = peers[offset]
+        block = f * near + n
+        loads[offset] = own(len(local) + i, keys.at[block], held_keys.at[block])
+        loads[offset].start()
+
+    barrier = pltpu.get_barrier_semaphore()
+    for offset in one_link + two_links:
+        greet = jnp.logical_or(
+            jnp.logical_and(role == ROOT, roles[offset] != END),
+            jnp.logical_or(
+                jnp.logical_and(role == SIDE, roles[offset] != SIDE),
+                jnp.logical_and(role == END, roles[offset] == END),
+            ),
+        )
+
+        @pl.when(greet)
+        def _(device=peers[offset]):
+            pl.semaphore_signal(barrier, inc=1, device_id=place_of(device), device_id_type=MESH)
+
     local[2].start()
-
-    barrier = pltpu.get_barrier_semaphore()
-    beside = [device for device, offset in zip(peers, offsets) if offset in one_link]
-    for device in beside:
-        pl.semaphore_signal(barrier, inc=1, device_id=place_of(device), device_id_type=MESH)
-    local[2].wait()
-    pl.semaphore_wait(barrier, len(beside))
-    same_far = [device for device, (f, n) in zip(peers, offsets) if f == 0]
-    for device in same_far:
-        pl.semaphore_signal(ready, inc=1, device_id=place_of(device), device_id_type=MESH)
-
     sends = {}
     for i, (source, target) in enumerate(((held_keys, landed), (values, out_values))):
-        for offset, (f, n) in zip(offsets, peers):
+        for offset in offsets:
+            f, n = peers[offset]
             sends[i, offset] = pltpu.make_async_remote_copy(
                 src_ref=source.at[f * near + n],
                 dst_ref=target.at[me],
@@ -87,16 +105,49 @@
                 device_id=place_of((f, n)),
                 device_id_type=MESH,
             )
-    for i, batch in ((0, one_link), (0, two_links), (1, two_links), (1, one_link)):
-        if (i, batch) == (0, two_links):
-            pl.semaphore_wait(ready, len(same_far))
-        for offset in batch:
-            sends[i, offset].start()
+
+    def tell(chosen):
+        for offset in one_link + two_links:
+
+            @pl.when(chosen(roles[offset]))
+            def _(device=peers[offset]):
+                pl.semaphore_signal(ready, inc=1, device_id=place_of(device), device_id_type=MESH)
+
+    def send_keys(offset):
+        loads[offset].wait()
+        sends[0, offset].start()
+
+    @pl.when(role == SIDE)
+    def _():
+        pl.semaphore_wait(barrier, roots)
+        for offset in one_link:
+            pl.when(roles[offset] == ROOT)(functools.partial(send_keys, offset))
+        pl.semaphore_wait(ready, ends)
+        tell(lambda other: other != SIDE)
+        for offset in one_link:
+            pl.when(roles[offset] != ROOT)(functools.partial(send_keys, offset))
+
+    @pl.when(role != SIDE)
+    def _():
+        pl.semaphore_wait(barrier, jnp.where(role == ROOT, roots, ends) - 1 + sides)
+
+        @pl.when(role == END)
+        def _():
+            tell(lambda other: other == SIDE)
+
+        for offset in one_link:
+            send_keys(offset)
+        pl.semaphore_wait(ready, sides)
+
+    for offset in two_links:
+        send_keys(offset)
+    for offset in two_links + one_link:
+        sends[1, offset].start()
 
     for copy in (local[0], local[1], local[3]):
         copy.start()
-    local[0].wait()
-    local[1].wait()
+    for copy in local[:3]:
+        copy.wait()
 
     @pl.loop(0, angles.shape[1] // LANES)
     def _(step):
@@ -131,7 +182,7 @@
     most = jnp.zeros((SUBLANES, LANES), jnp.float32)
     most = turn_block(held_keys, me, most)
     for offset in one_link + two_links:
-        f, n = peers[offsets.index(offset)]
+        f, n = peers[offset]
         sends[0, offset].wait_recv()
         most = turn_block(landed, f * near + n, most)
     scale = most[:heads]
@@ -174,7 +225,7 @@
     batch, length, heads, size = raw_keys.shape
     members = far * near
     assert batch == members and size == LANES and SUBLANES % heads == 0
-    assert far & (far - 1) == 0 and near & (near - 1) == 0
+    assert far > 2 and near > 1 and far & (far - 1) == 0 and near & (near - 1) == 0
     rows = length * heads
     offsets = [(f, n) for f in range(far) for n in range(near) if (f, n) != (0, 0)]
     offsets.sort(key=lambda o: (o[0] < 2 and o[1] == 0, o[1], o[0]))
@@ -199,7 +250,7 @@
             pltpu.VMEM((1, size), jnp.float32),
             pltpu.SemaphoreType.DMA((2, len(offsets))),
             pltpu.SemaphoreType.DMA((2, len(offsets))),
-            pltpu.SemaphoreType.DMA((4,)),
+            pltpu.SemaphoreType.DMA((4 + len(offsets),)),
             pltpu.SemaphoreType.REGULAR,
         ],
         compiler_params=pltpu.CompilerParams(

time: 30 us -> 29.1 us (0.970)
  Pallas kernels: 29.1 us -> 28.1 us
    pallas_call x1, Pallas kernels: 27.8 us -> 26.8 us  [shards(): pl.pallas_call(functools.partial(kernel, far, near, heads, offsets), out_...]
where the time goes in v1:
time: 29.1 us; the launch traced here: 28.7 us
  Pallas kernels  28.1 us (97%)
  between operations  0.64 us (2%)
    pallas_call x1, Pallas kernels, shards(): pl.pallas_call(functools.partial(kernel, far, near, heads, offsets), out_...  26.8 us
    pallas_call x1, Pallas kernels, shards(): pl.pallas_call(write_out, out_shape=tuple((pltpu.HBM(r.shape, r.dtype) fo...  1.35 us

profile of v1, /device:TPU:0, one launch (start us, length us, event | category | flops | bytes accessed | tf_op | source)
XLA Modules:
  0.0 28.7 jit_solution(6487997084584982905)
XLA Ops:
  0.6 26.8 %move_and_turn.1 = (bf16[4096,128]{1,0:T(8,128)(2,1)S(1)}, bf16[8,512,128]{2,1,0:T(8,128)(2,1)S(1)}, f32[2,128]{1,0:T(2,128)S(1)}) custom-call(bf16[8,512,128]{2,1,0:T(8,128)(2,1)} %bitcast.7, bf16[8,512,128]{2,1,0:T(8,128)(2,1)} %bitcast.8, f32[64,2048]{1,0:T(8,128)} %bitcast.9, f32[1,128]{1,0:T(1,128)} %bitcast.10), custom_call_target="tpu_custom_call" | custom-call | tf_op jit(solution)/shard_map/move_and_turn/pallas_call | solution.py:234
  27.4 1.3 %write_out.1 = (bf16[4096,128]{1,0:T(8,128)(2,1)}, bf16[8,512,128]{2,1,0:T(8,128)(2,1)}, f32[2,128]{1,0:T(2,128)}) custom-call(bf16[4096,128]{1,0:T(8,128)(2,1)S(1)} %get-tuple-element.9.refs_0_, bf16[8,512,128]{2,1,0:T(8,128)(2,1)S(1)} %get-tuple-element.10.refs_1_, f32[2,128]{1,0:T(2,128)S(1)} %get-tuple-element.11.refs_2_), custom_call_target="tpu_custom_call" | custom-call | tf_op jit(solution)/shard_map/write_out/pallas_call | solution.py:266

commit v2 on v1

--- a/solution.py
+++ b/solution.py
@@ -71,40 +71,59 @@
         own(2, keys.at[me], held_keys.at[me]),
         own(3, values.at[me], out_values.at[me]),
     ]
-    loads = {}
-    for i, offset in enumerate(one_link + two_links):
+    head = rows // 4
+    first = ((2, 0), (0, 1))
+    pieces = {o: (pl.ds(0, rows),) for o in one_link + two_links}
+    for offset in first:
+        pieces[offset] = (pl.ds(0, head), pl.ds(head, rows - head))
+
+    def send(i, source, target, offset, place):
         f, n = peers[offset]
-        block = f * near + n
-        loads[offset] = own(len(local) + i, keys.at[block], held_keys.at[block])
-        loads[offset].start()
+        return pltpu.make_async_remote_copy(
+            src_ref=source.at[f * near + n, place],
+            dst_ref=target.at[me, place],
+            send_sem=send_sem.at[i, offsets.index(offset)],
+            recv_sem=recv_sem.at[i, offsets.index(offset)],
+            device_id=place_of((f, n)),
+            device_id_type=MESH,
+        )
+
+    sends, loads = {}, {}
+    for i, (source, target) in enumerate(((held_keys, landed), (values, out_values))):
+        for offset in offsets:
+            sends[i, offset] = send(i, source, target, offset, pl.ds(0, rows))
+    for offset in one_link + two_links:
+        f, n = peers[offset]
+        for part, piece in enumerate(pieces[offset]):
+            place = (f * near + n, piece)
+            loads[offset, part] = own(len(local) + len(loads), keys.at[place], held_keys.at[place])
 
     barrier = pltpu.get_barrier_semaphore()
     for offset in one_link + two_links:
         greet = jnp.logical_or(
             jnp.logical_and(role == ROOT, roles[offset] != END),
-            jnp.logical_or(
-                jnp.logical_and(role == SIDE, roles[offset] != SIDE),
-                jnp.logical_and(role == END, roles[offset] == END),
-            ),
+            jnp.logical_and(role == SIDE, roles[offset] != SIDE),
         )
 
         @pl.when(greet)
         def _(device=peers[offset]):
             pl.semaphore_signal(barrier, inc=1, device_id=place_of(device), device_id_type=MESH)
 
+    straight = {o: jnp.logical_and(role == SIDE, roles[o] == ROOT) for o in one_link}
+
+    @pl.when(role == SIDE)
+    def _():
+        pl.semaphore_wait(barrier, roots)
+        for offset in sorted(one_link, key=lambda o: -o[0]):
+            pl.when(straight[offset])(send(0, keys, landed, offset, pl.ds(0, rows)).start)
+
+    for offset, part in sorted(loads, key=lambda at: (at[0] not in first, at[1])):
+        load = loads[offset, part].start
+        if offset in straight:
+            pl.when(jnp.logical_not(straight[offset]))(load)
+        else:
+            load()
     local[2].start()
-    sends = {}
-    for i, (source, target) in enumerate(((held_keys, landed), (values, out_values))):
-        for offset in offsets:
-            f, n = peers[offset]
-            sends[i, offset] = pltpu.make_async_remote_copy(
-                src_ref=source.at[f * near + n],
-                dst_ref=target.at[me],
-                send_sem=send_sem.at[i, offsets.index(offset)],
-                recv_sem=recv_sem.at[i, offsets.index(offset)],
-                device_id=place_of((f, n)),
-                device_id_type=MESH,
-            )
 
     def tell(chosen):
         for offset in one_link + two_links:
@@ -114,30 +133,32 @@
                 pl.semaphore_signal(ready, inc=1, device_id=place_of(device), device_id_type=MESH)
 
     def send_keys(offset):
-        loads[offset].wait()
-        sends[0, offset].start()
+        for part, place in enumerate(pieces[offset]):
+            loads[offset, part].wait()
+            send(0, held_keys, landed, offset, place).start()
 
     @pl.when(role == SIDE)
     def _():
-        pl.semaphore_wait(barrier, roots)
+        pl.semaphore_wait(ready, ends)
         for offset in one_link:
-            pl.when(roles[offset] == ROOT)(functools.partial(send_keys, offset))
-        pl.semaphore_wait(ready, ends)
+            pl.when(roles[offset] == END)(functools.partial(send_keys, offset))
         tell(lambda other: other != SIDE)
         for offset in one_link:
-            pl.when(roles[offset] != ROOT)(functools.partial(send_keys, offset))
+            pl.when(roles[offset] == SIDE)(functools.partial(send_keys, offset))
 
     @pl.when(role != SIDE)
     def _():
-        pl.semaphore_wait(barrier, jnp.where(role == ROOT, roots, ends) - 1 + sides)
+        pl.semaphore_wait(barrier, jnp.where(role == ROOT, roots - 1, 0) + sides)
 
         @pl.when(role == END)
         def _():
             tell(lambda other: other == SIDE)
 
         for offset in one_link:
-            send_keys(offset)
+            pl.when(roles[offset] == SIDE)(functools.partial(send_keys, offset))
         pl.semaphore_wait(ready, sides)
+        for offset in one_link:
+            pl.when(roles[offset] != SIDE)(functools.partial(send_keys, offset))
 
     for offset in two_links:
         send_keys(offset)
@@ -200,8 +221,8 @@
     local[3].wait()
     for offset in offsets:
         sends[1, offset].wait_recv()
-    for send in sends.values():
-        send.wait_send()
+    for sent in sends.values():
+        sent.wait_send()
 
 
 def hold(x):
@@ -250,7 +271,7 @@
             pltpu.VMEM((1, size), jnp.float32),
             pltpu.SemaphoreType.DMA((2, len(offsets))),
             pltpu.SemaphoreType.DMA((2, len(offsets))),
-            pltpu.SemaphoreType.DMA((4 + len(offsets),)),
+            pltpu.SemaphoreType.DMA((6 + len(offsets),)),
             pltpu.SemaphoreType.REGULAR,
         ],
         compiler_params=pltpu.CompilerParams(

time: 29.1 us -> 28.8 us (0.990)
  no operation moved by 1% of the time
where the time goes in v2:
time: 28.8 us; the launch traced here: 28.6 us
  Pallas kernels  28 us (97%)
  between operations  0.64 us (2%)
    pallas_call x1, Pallas kernels, shards(): pl.pallas_call(functools.partial(kernel, far, near, heads, offsets), out_...  26.6 us
    pallas_call x1, Pallas kernels, shards(): pl.pallas_call(write_out, out_shape=tuple((pltpu.HBM(r.shape, r.dtype) fo...  1.35 us

profile of v2, /device:TPU:0, one launch (start us, length us, event | category | flops | bytes accessed | tf_op | source)
XLA Modules:
  0.0 28.6 jit_solution(15610525409356326167)
XLA Ops:
  0.6 26.6 %move_and_turn.1 = (bf16[4096,128]{1,0:T(8,128)(2,1)S(1)}, bf16[8,512,128]{2,1,0:T(8,128)(2,1)S(1)}, f32[2,128]{1,0:T(2,128)S(1)}) custom-call(bf16[8,512,128]{2,1,0:T(8,128)(2,1)} %bitcast.7, bf16[8,512,128]{2,1,0:T(8,128)(2,1)} %bitcast.8, f32[64,2048]{1,0:T(8,128)} %bitcast.9, f32[1,128]{1,0:T(1,128)} %bitcast.10), custom_call_target="tpu_custom_call" | custom-call | tf_op jit(solution)/shard_map/move_and_turn/pallas_call | solution.py:255
  27.3 1.3 %write_out.1 = (bf16[4096,128]{1,0:T(8,128)(2,1)}, bf16[8,512,128]{2,1,0:T(8,128)(2,1)}, f32[2,128]{1,0:T(2,128)}) custom-call(bf16[4096,128]{1,0:T(8,128)(2,1)S(1)} %get-tuple-element.9.refs_0_, bf16[8,512,128]{2,1,0:T(8,128)(2,1)S(1)} %get-tuple-element.10.refs_1_, f32[2,128]{1,0:T(2,128)S(1)} %get-tuple-element.11.refs_2_), custom_call_target="tpu_custom_call" | custom-call | tf_op jit(solution)/shard_map/write_out/pallas_call | solution.py:287

commit v3 on v2

--- a/solution.py
+++ b/solution.py
@@ -50,7 +50,8 @@
 
 
 def kernel(far, near, heads, offsets, keys, values, angle, gain, out_keys, out_values, out_scale,
-           landed, held_keys, turned, cosines, sines, angles, gains, send_sem, recv_sem, local_sem, ready):
+           landed, held_keys, turned, cosines, sines, angles, gains, send_sem, recv_sem, local_sem,
+           ready, link):
     members, rows, _ = landed.shape
     far_index, near_index = lax.axis_index("farcp"), lax.axis_index("nearcp")
     me = far_index * near + near_index
@@ -60,7 +61,11 @@
         (f, n): (partner(far_index, f, far), partner(near_index, n, near)) for f, n in offsets
     }
     role, roles = role_of(far_index, near_index), {o: role_of(*peers[o]) for o in offsets}
-    roots, sides, ends = 2, 2 * (near - 1) + far - 2, (far - 2) * (near - 1)
+    core = far_index % 2
+    odd, mate = core == 1, (far_index + 1 - 2 * core, near_index)
+    roots = [(f, 0) for f in range(2)]
+    sides = [(f, n) for f in range(2) for n in range(1, near)] + [(f, 0) for f in range(2, far)]
+    ends = [(f, n) for f in range(2, far) for n in range(1, near)]
 
     def own(i, source, target):
         return pltpu.make_async_copy(source, target, local_sem.at[i])
@@ -82,8 +87,8 @@
         return pltpu.make_async_remote_copy(
             src_ref=source.at[f * near + n, place],
             dst_ref=target.at[me, place],
-            send_sem=send_sem.at[i, offsets.index(offset)],
-            recv_sem=recv_sem.at[i, offsets.index(offset)],
+            send_sem=send_sem.at[i, offset[0] * near + offset[1]],
+            recv_sem=recv_sem.at[i, offset[0] * near + offset[1]],
             device_id=place_of((f, n)),
             device_id_type=MESH,
         )
@@ -98,25 +103,48 @@
             place = (f * near + n, piece)
             loads[offset, part] = own(len(local) + len(loads), keys.at[place], held_keys.at[place])
 
+    def tell(semaphore, devices):
+        for device in devices:
+            pl.semaphore_signal(
+                semaphore, inc=1, device_id=place_of(device), device_id_type=MESH
+            )
+
+    def send_straight():
+        for root, far_step in ((1 - core, far_index + 1 - core), (core, far_index - core)):
+            pltpu.make_async_remote_copy(
+                src_ref=keys.at[root * near],
+                dst_ref=landed.at[me],
+                send_sem=send_sem.at[0, far_step * near + near_index],
+                recv_sem=recv_sem.at[0, far_step * near + near_index],
+                device_id=place_of((root, 0)),
+                device_id_type=MESH,
+            ).start()
+
     barrier = pltpu.get_barrier_semaphore()
-    for offset in one_link + two_links:
-        greet = jnp.logical_or(
-            jnp.logical_and(role == ROOT, roles[offset] != END),
-            jnp.logical_and(role == SIDE, roles[offset] != SIDE),
-        )
-
-        @pl.when(greet)
-        def _(device=peers[offset]):
-            pl.semaphore_signal(barrier, inc=1, device_id=place_of(device), device_id_type=MESH)
+
+    @pl.when(role == SIDE)
+    def _():
+        @pl.when(odd)
+        def _():
+            tell(barrier, roots)
+
+        tell(barrier, ends)
+
+        @pl.when(odd)
+        def _():
+            tell(barrier, [mate])
+            pl.semaphore_wait(barrier, len(roots))
+            send_straight()
+
+    @pl.when(role == ROOT)
+    def _():
+        tell(barrier, [mate] + [d for d in sides if d[0] % 2 == 1])
+
+    @pl.when(role == END)
+    def _():
+        tell(barrier, [d for d in sides if d[0] % 2 == 0])
 
     straight = {o: jnp.logical_and(role == SIDE, roles[o] == ROOT) for o in one_link}
-
-    @pl.when(role == SIDE)
-    def _():
-        pl.semaphore_wait(barrier, roots)
-        for offset in sorted(one_link, key=lambda o: -o[0]):
-            pl.when(straight[offset])(send(0, keys, landed, offset, pl.ds(0, rows)).start)
-
     for offset, part in sorted(loads, key=lambda at: (at[0] not in first, at[1])):
         load = loads[offset, part].start
         if offset in straight:
@@ -125,45 +153,70 @@
             load()
     local[2].start()
 
-    def tell(chosen):
-        for offset in one_link + two_links:
-
-            @pl.when(chosen(roles[offset]))
-            def _(device=peers[offset]):
-                pl.semaphore_signal(ready, inc=1, device_id=place_of(device), device_id_type=MESH)
-
     def send_keys(offset):
         for part, place in enumerate(pieces[offset]):
             loads[offset, part].wait()
             send(0, held_keys, landed, offset, place).start()
 
+    def send_to(chosen):
+        for offset in one_link:
+            pl.when(chosen(roles[offset]))(functools.partial(send_keys, offset))
+
     @pl.when(role == SIDE)
     def _():
-        pl.semaphore_wait(ready, ends)
-        for offset in one_link:
-            pl.when(roles[offset] == END)(functools.partial(send_keys, offset))
-        tell(lambda other: other != SIDE)
-        for offset in one_link:
-            pl.when(roles[offset] == SIDE)(functools.partial(send_keys, offset))
-
-    @pl.when(role != SIDE)
-    def _():
-        pl.semaphore_wait(barrier, jnp.where(role == ROOT, roots - 1, 0) + sides)
-
-        @pl.when(role == END)
-        def _():
-            tell(lambda other: other == SIDE)
-
-        for offset in one_link:
-            pl.when(roles[offset] == SIDE)(functools.partial(send_keys, offset))
-        pl.semaphore_wait(ready, sides)
-        for offset in one_link:
-            pl.when(roles[offset] != SIDE)(functools.partial(send_keys, offset))
+        @pl.when(odd)
+        def _():
+            pl.semaphore_wait(link, 1)
+
+        @pl.when(jnp.logical_not(odd))
+        def _():
+            pl.semaphore_wait(barrier, len(ends) + 1)
+
+        tell(link, [mate])
+
+        @pl.when(jnp.logical_not(odd))
+        def _():
+            pl.semaphore_wait(link, 1)
+            send_straight()
+
+        send_to(lambda other: other == END)
+
+        tell(ready, roots + ends)
+        pl.semaphore_wait(ready, 1)
+        send_to(lambda other: other == SIDE)
+
+    @pl.when(role == ROOT)
+    def _():
+        pl.semaphore_wait(barrier, len(roots) - 1 + len(sides) // 2)
+        for wanted in (1, 0):
+            for offset in one_link:
+                chosen = jnp.logical_and(roles[offset] == SIDE, peers[offset][0] % 2 == wanted)
+                pl.when(chosen)(functools.partial(send_keys, offset))
+            if wanted:
+                pl.semaphore_wait(ready, len(sides))
+                tell(ready, [(d[0] + core, d[1]) for d in sides if d[0] % 2 == 0])
+        send_to(lambda other: other == ROOT)
+
+    @pl.when(role == END)
+    def _():
+        pl.semaphore_wait(barrier, len(sides))
+        send_to(lambda other: other == SIDE)
+        pl.semaphore_wait(ready, len(sides))
+        send_to(lambda other: other == END)
 
     for offset in two_links:
         send_keys(offset)
-    for offset in two_links + one_link:
+    inner = jnp.logical_and(role == SIDE, near_index == 0)
+    across = [o for o in one_link if o[0] >= 2]
+    for offset in across:
+        pl.when(inner)(sends[1, offset].start)
+    for offset in two_links:
         sends[1, offset].start()
+    for offset in across:
+        pl.when(jnp.logical_not(inner))(sends[1, offset].start)
+    for offset in one_link:
+        if offset not in across:
+            sends[1, offset].start()
 
     for copy in (local[0], local[1], local[3]):
         copy.start()
@@ -202,7 +255,7 @@
 
     most = jnp.zeros((SUBLANES, LANES), jnp.float32)
     most = turn_block(held_keys, me, most)
-    for offset in one_link + two_links:
+    for offset in sorted(one_link + two_links, key=lambda o: o[0] == 1 and o[1] > 0):
         f, n = peers[offset]
         sends[0, offset].wait_recv()
         most = turn_block(landed, f * near + n, most)
@@ -269,9 +322,10 @@
             pltpu.VMEM((members * rows, size), jnp.float32),
             pltpu.VMEM((size // 2, members * length), jnp.float32),
             pltpu.VMEM((1, size), jnp.float32),
-            pltpu.SemaphoreType.DMA((2, len(offsets))),
-            pltpu.SemaphoreType.DMA((2, len(offsets))),
+            pltpu.SemaphoreType.DMA((2, members)),
+            pltpu.SemaphoreType.DMA((2, members)),
             pltpu.SemaphoreType.DMA((6 + len(offsets),)),
+            pltpu.SemaphoreType.REGULAR,
             pltpu.SemaphoreType.REGULAR,
         ],
         compiler_params=pltpu.CompilerParams(

time: 28.8 us -> 28.6 us (level); the launches traced: 28.6 us -> 28.1 us
  Pallas kernels: 28 us -> 27.4 us
    pallas_call x1, Pallas kernels: 26.6 us -> 26.1 us  [shards(): pl.pallas_call(functools.partial(kernel, far, near, heads, offsets), out_...]
where the time goes in v3:
time: 28.6 us; the launch traced here: 28.1 us
  Pallas kernels  27.4 us (96%)
  between operations  0.64 us (2%)
    pallas_call x1, Pallas kernels, shards(): pl.pallas_call(functools.partial(kernel, far, near, heads, offsets), out_...  26.1 us
    pallas_call x1, Pallas kernels, shards(): pl.pallas_call(write_out, out_shape=tuple((pltpu.HBM(r.shape, r.dtype) fo...  1.35 us

profile of v3, /device:TPU:0, one launch (start us, length us, event | category | flops | bytes accessed | tf_op | source)
XLA Modules:
  0.0 28.1 jit_solution(4616614385351710164)
XLA Ops:
  0.6 26.1 %move_and_turn.1 = (bf16[4096,128]{1,0:T(8,128)(2,1)S(1)}, bf16[8,512,128]{2,1,0:T(8,128)(2,1)S(1)}, f32[2,128]{1,0:T(2,128)S(1)}) custom-call(bf16[8,512,128]{2,1,0:T(8,128)(2,1)} %bitcast.7, bf16[8,512,128]{2,1,0:T(8,128)(2,1)} %bitcast.8, f32[64,2048]{1,0:T(8,128)} %bitcast.9, f32[1,128]{1,0:T(1,128)} %bitcast.10), custom_call_target="tpu_custom_call" | custom-call | tf_op jit(solution)/shard_map/move_and_turn/pallas_call | solution.py:308
  26.7 1.3 %write_out.1 = (bf16[4096,128]{1,0:T(8,128)(2,1)}, bf16[8,512,128]{2,1,0:T(8,128)(2,1)}, f32[2,128]{1,0:T(2,128)}) custom-call(bf16[4096,128]{1,0:T(8,128)(2,1)S(1)} %get-tuple-element.9.refs_0_, bf16[8,512,128]{2,1,0:T(8,128)(2,1)S(1)} %get-tuple-element.10.refs_1_, f32[2,128]{1,0:T(2,128)S(1)} %get-tuple-element.11.refs_2_), custom_call_target="tpu_custom_call" | custom-call | tf_op jit(solution)/shard_map/write_out/pallas_call | solution.py:341

commit v4 on v3

--- a/solution.py
+++ b/solution.py
@@ -51,7 +51,7 @@
 
 def kernel(far, near, heads, offsets, keys, values, angle, gain, out_keys, out_values, out_scale,
            landed, held_keys, turned, cosines, sines, angles, gains, send_sem, recv_sem, local_sem,
-           ready, link):
+           ready, link, more):
     members, rows, _ = landed.shape
     far_index, near_index = lax.axis_index("farcp"), lax.axis_index("nearcp")
     me = far_index * near + near_index
@@ -142,7 +142,13 @@
 
     @pl.when(role == END)
     def _():
-        tell(barrier, [d for d in sides if d[0] % 2 == 0])
+        @pl.when(odd)
+        def _():
+            tell(barrier, [d for d in sides if d[0] % 2 == 0])
+
+        @pl.when(jnp.logical_not(odd))
+        def _():
+            tell(barrier, [mate])
 
     straight = {o: jnp.logical_and(role == SIDE, roles[o] == ROOT) for o in one_link}
     for offset, part in sorted(loads, key=lambda at: (at[0] not in first, at[1])):
@@ -158,9 +164,12 @@
             loads[offset, part].wait()
             send(0, held_keys, landed, offset, place).start()
 
-    def send_to(chosen):
+    def send_to(other, *cores):
         for offset in one_link:
-            pl.when(chosen(roles[offset]))(functools.partial(send_keys, offset))
+            chosen = roles[offset] == other
+            for wanted in cores:
+                chosen = jnp.logical_and(chosen, peers[offset][0] % 2 == wanted)
+            pl.when(chosen)(functools.partial(send_keys, offset))
 
     @pl.when(role == SIDE)
     def _():
@@ -170,39 +179,38 @@
 
         @pl.when(jnp.logical_not(odd))
         def _():
-            pl.semaphore_wait(barrier, len(ends) + 1)
+            pl.semaphore_wait(barrier, len(ends) // 2 + 1)
 
         tell(link, [mate])
+        send_to(END, 1)
 
         @pl.when(jnp.logical_not(odd))
         def _():
             pl.semaphore_wait(link, 1)
             send_straight()
 
-        send_to(lambda other: other == END)
-
+        pl.semaphore_wait(more, len(ends) // 2)
+        send_to(END, 0)
         tell(ready, roots + ends)
         pl.semaphore_wait(ready, 1)
-        send_to(lambda other: other == SIDE)
+        send_to(SIDE)
 
     @pl.when(role == ROOT)
     def _():
         pl.semaphore_wait(barrier, len(roots) - 1 + len(sides) // 2)
-        for wanted in (1, 0):
-            for offset in one_link:
-                chosen = jnp.logical_and(roles[offset] == SIDE, peers[offset][0] % 2 == wanted)
-                pl.when(chosen)(functools.partial(send_keys, offset))
-            if wanted:
-                pl.semaphore_wait(ready, len(sides))
-                tell(ready, [(d[0] + core, d[1]) for d in sides if d[0] % 2 == 0])
-        send_to(lambda other: other == ROOT)
+        send_to(SIDE, 1)
+        pl.semaphore_wait(ready, len(sides))
+        tell(ready, [(d[0] + core, d[1]) for d in sides if d[0] % 2 == 0])
+        send_to(SIDE, 0)
+        send_to(ROOT)
 
     @pl.when(role == END)
     def _():
-        pl.semaphore_wait(barrier, len(sides))
-        send_to(lambda other: other == SIDE)
+        pl.semaphore_wait(barrier, len(sides) + core)
+        pl.when(odd)(functools.partial(tell, more, sides))
+        send_to(SIDE)
         pl.semaphore_wait(ready, len(sides))
-        send_to(lambda other: other == END)
+        send_to(END)
 
     for offset in two_links:
         send_keys(offset)
@@ -327,6 +335,7 @@
             pltpu.SemaphoreType.DMA((6 + len(offsets),)),
             pltpu.SemaphoreType.REGULAR,
             pltpu.SemaphoreType.REGULAR,
+            pltpu.SemaphoreType.REGULAR,
         ],
         compiler_params=pltpu.CompilerParams(
             collective_id=0, has_side_effects=True, vmem_limit_bytes=32 * 1024 * 1024

time: 28.6 us -> 28.4 us (level)
  no operation moved by 1% of the time
where the time goes in v4:
time: 28.4 us; the launch traced here: 28.1 us
  Pallas kernels  27.4 us (96%)
  between operations  0.64 us (2%)
    pallas_call x1, Pallas kernels, shards(): pl.pallas_call(functools.partial(kernel, far, near, heads, offsets), out_...  26.1 us
    pallas_call x1, Pallas kernels, shards(): pl.pallas_call(write_out, out_shape=tuple((pltpu.HBM(r.shape, r.dtype) fo...  1.35 us

profile of v4, /device:TPU:0, one launch (start us, length us, event | category | flops | bytes accessed | tf_op | source)
XLA Modules:
  0.0 28.1 jit_solution(15260334449511305027)
XLA Ops:
  0.6 26.1 %move_and_turn.1 = (bf16[4096,128]{1,0:T(8,128)(2,1)S(1)}, bf16[8,512,128]{2,1,0:T(8,128)(2,1)S(1)}, f32[2,128]{1,0:T(2,128)S(1)}) custom-call(bf16[8,512,128]{2,1,0:T(8,128)(2,1)} %bitcast.7, bf16[8,512,128]{2,1,0:T(8,128)(2,1)} %bitcast.8, f32[64,2048]{1,0:T(8,128)} %bitcast.9, f32[1,128]{1,0:T(1,128)} %bitcast.10), custom_call_target="tpu_custom_call" | custom-call | tf_op jit(solution)/shard_map/move_and_turn/pallas_call | solution.py:316
  26.7 1.3 %write_out.1 = (bf16[4096,128]{1,0:T(8,128)(2,1)}, bf16[8,512,128]{2,1,0:T(8,128)(2,1)}, f32[2,128]{1,0:T(2,128)}) custom-call(bf16[4096,128]{1,0:T(8,128)(2,1)S(1)} %get-tuple-element.9.refs_0_, bf16[8,512,128]{2,1,0:T(8,128)(2,1)S(1)} %get-tuple-element.10.refs_1_, f32[2,128]{1,0:T(2,128)S(1)} %get-tuple-element.11.refs_2_), custom_call_target="tpu_custom_call" | custom-call | tf_op jit(solution)/shard_map/write_out/pallas_call | solution.py:350

commit v5 on v4

--- a/solution.py
+++ b/solution.py
@@ -215,16 +215,23 @@
     for offset in two_links:
         send_keys(offset)
     inner = jnp.logical_and(role == SIDE, near_index == 0)
-    across = [o for o in one_link if o[0] >= 2]
-    for offset in across:
-        pl.when(inner)(sends[1, offset].start)
+    outward = jnp.logical_and(role != SIDE, jnp.logical_not(odd))
+    pairs = [(o, (o[0] + 1, o[1])) for o in one_link if o[0] % 2 == 0]
+    across = [pair for pair in pairs if pair[0][0] >= 2]
+
+    def send_values(chosen):
+        for low, high in chosen:
+            swap = jnp.logical_and(outward, roles[low] == SIDE)
+            pl.when(swap)(sends[1, high].start)
+            sends[1, low].start()
+            pl.when(jnp.logical_not(swap))(sends[1, high].start)
+
+    pl.when(inner)(functools.partial(send_values, across))
     for offset in two_links:
         sends[1, offset].start()
-    for offset in across:
-        pl.when(jnp.logical_not(inner))(sends[1, offset].start)
-    for offset in one_link:
-        if offset not in across:
-            sends[1, offset].start()
+    pl.when(jnp.logical_not(inner))(functools.partial(send_values, across))
+    send_values([pair for pair in pairs if pair not in across])
+    sends[1, (1, 0)].start()
 
     for copy in (local[0], local[1], local[3]):
         copy.start()

time: 28.4 us -> 28.4 us (level)
  no operation moved by 1% of the time
where the time goes in v5:
time: 28.4 us; the launch traced here: 28.1 us
  Pallas kernels  27.4 us (96%)
  between operations  0.64 us (2%)
    pallas_call x1, Pallas kernels, shards(): pl.pallas_call(functools.partial(kernel, far, near, heads, offsets), out_...  26.1 us
    pallas_call x1, Pallas kernels, shards(): pl.pallas_call(write_out, out_shape=tuple((pltpu.HBM(r.shape, r.dtype) fo...  1.35 us

profile of v5, /device:TPU:0, one launch (start us, length us, event | category | flops | bytes accessed | tf_op | source)
XLA Modules:
  0.0 28.1 jit_solution(12416108642457336869)
XLA Ops:
  0.6 26.1 %move_and_turn.1 = (bf16[4096,128]{1,0:T(8,128)(2,1)S(1)}, bf16[8,512,128]{2,1,0:T(8,128)(2,1)S(1)}, f32[2,128]{1,0:T(2,128)S(1)}) custom-call(bf16[8,512,128]{2,1,0:T(8,128)(2,1)} %bitcast.7, bf16[8,512,128]{2,1,0:T(8,128)(2,1)} %bitcast.8, f32[64,2048]{1,0:T(8,128)} %bitcast.9, f32[1,128]{1,0:T(1,128)} %bitcast.10), custom_call_target="tpu_custom_call" | custom-call | tf_op jit(solution)/shard_map/move_and_turn/pallas_call | solution.py:323
  26.7 1.3 %write_out.1 = (bf16[4096,128]{1,0:T(8,128)(2,1)}, bf16[8,512,128]{2,1,0:T(8,128)(2,1)}, f32[2,128]{1,0:T(2,128)}) custom-call(bf16[4096,128]{1,0:T(8,128)(2,1)S(1)} %get-tuple-element.9.refs_0_, bf16[8,512,128]{2,1,0:T(8,128)(2,1)S(1)} %get-tuple-element.10.refs_1_, f32[2,128]{1,0:T(2,128)S(1)} %get-tuple-element.11.refs_2_), custom_call_target="tpu_custom_call" | custom-call | tf_op jit(solution)/shard_map/write_out/pallas_call | solution.py:357

commit v6 on v5

--- a/solution.py
+++ b/solution.py
@@ -127,19 +127,29 @@
         @pl.when(odd)
         def _():
             tell(barrier, roots)
-
-        tell(barrier, ends)
-
-        @pl.when(odd)
-        def _():
-            tell(barrier, [mate])
             pl.semaphore_wait(barrier, len(roots))
             send_straight()
+            tell(barrier, [mate])
+
+        tell(barrier, ends)
 
     @pl.when(role == ROOT)
     def _():
         tell(barrier, [mate] + [d for d in sides if d[0] % 2 == 1])
 
+    straight = {o: jnp.logical_and(role == SIDE, roles[o] == ROOT) for o in one_link}
+
+    def start_loads(chosen):
+        for offset, part in chosen:
+            load = loads[offset, part].start
+            if offset in straight:
+                pl.when(jnp.logical_not(straight[offset]))(load)
+            else:
+                load()
+
+    queue = sorted(loads, key=lambda at: (at[0] not in first, at[1]))
+    start_loads(queue[:2])
+
     @pl.when(role == END)
     def _():
         @pl.when(odd)
@@ -150,13 +160,7 @@
         def _():
             tell(barrier, [mate])
 
-    straight = {o: jnp.logical_and(role == SIDE, roles[o] == ROOT) for o in one_link}
-    for offset, part in sorted(loads, key=lambda at: (at[0] not in first, at[1])):
-        load = loads[offset, part].start
-        if offset in straight:
-            pl.when(jnp.logical_not(straight[offset]))(load)
-        else:
-            load()
+    start_loads(queue[2:])
     local[2].start()
 
     def send_keys(offset):

time: 28.4 us -> 28.4 us (level)
  no operation moved by 1% of the time
where the time goes in v6:
time: 28.4 us; the launch traced here: 28.1 us
  Pallas kernels  27.4 us (96%)
  between operations  0.64 us (2%)
    pallas_call x1, Pallas kernels, shards(): pl.pallas_call(functools.partial(kernel, far, near, heads, offsets), out_...  26.1 us
    pallas_call x1, Pallas kernels, shards(): pl.pallas_call(write_out, out_shape=tuple((pltpu.HBM(r.shape, r.dtype) fo...  1.35 us

profile of v6, /device:TPU:0, one launch (start us, length us, event | category | flops | bytes accessed | tf_op | source)
XLA Modules:
  0.0 28.1 jit_solution(6019107145530368361)
XLA Ops:
  0.6 26.1 %move_and_turn.1 = (bf16[4096,128]{1,0:T(8,128)(2,1)S(1)}, bf16[8,512,128]{2,1,0:T(8,128)(2,1)S(1)}, f32[2,128]{1,0:T(2,128)S(1)}) custom-call(bf16[8,512,128]{2,1,0:T(8,128)(2,1)} %bitcast.7, bf16[8,512,128]{2,1,0:T(8,128)(2,1)} %bitcast.8, f32[64,2048]{1,0:T(8,128)} %bitcast.9, f32[1,128]{1,0:T(1,128)} %bitcast.10), custom_call_target="tpu_custom_call" | custom-call | tf_op jit(solution)/shard_map/move_and_turn/pallas_call | solution.py:327
  26.7 1.3 %write_out.1 = (bf16[4096,128]{1,0:T(8,128)(2,1)}, bf16[8,512,128]{2,1,0:T(8,128)(2,1)}, f32[2,128]{1,0:T(2,128)}) custom-call(bf16[4096,128]{1,0:T(8,128)(2,1)S(1)} %get-tuple-element.9.refs_0_, bf16[8,512,128]{2,1,0:T(8,128)(2,1)S(1)} %get-tuple-element.10.refs_1_, f32[2,128]{1,0:T(2,128)S(1)} %get-tuple-element.11.refs_2_), custom_call_target="tpu_custom_call" | custom-call | tf_op jit(solution)/shard_map/write_out/pallas_call | solution.py:361

commit v7 on v5

--- a/solution.py
+++ b/solution.py
@@ -221,7 +221,8 @@
 
     def send_values(chosen):
         for low, high in chosen:
-            swap = jnp.logical_and(outward, roles[low] == SIDE)
+            beside = jnp.logical_and(roles[low] == SIDE, peers[low][1] == 0)
+            swap = jnp.logical_and(outward, beside)
             pl.when(swap)(sends[1, high].start)
             sends[1, low].start()
             pl.when(jnp.logical_not(swap))(sends[1, high].start)

time: 28.4 us -> 28.4 us (level)
  no operation moved by 1% of the time
where the time goes in v7:
time: 28.4 us; the launch traced here: 28.1 us
  Pallas kernels  27.4 us (96%)
  between operations  0.64 us (2%)
    pallas_call x1, Pallas kernels, shards(): pl.pallas_call(functools.partial(kernel, far, near, heads, offsets), out_...  26.1 us
    pallas_call x1, Pallas kernels, shards(): pl.pallas_call(write_out, out_shape=tuple((pltpu.HBM(r.shape, r.dtype) fo...  1.35 us

profile of v7, /device:TPU:0, one launch (start us, length us, event | category | flops | bytes accessed | tf_op | source)
XLA Modules:
  0.0 28.1 jit_solution(18206216026678066693)
XLA Ops:
  0.6 26.1 %move_and_turn.1 = (bf16[4096,128]{1,0:T(8,128)(2,1)S(1)}, bf16[8,512,128]{2,1,0:T(8,128)(2,1)S(1)}, f32[2,128]{1,0:T(2,128)S(1)}) custom-call(bf16[8,512,128]{2,1,0:T(8,128)(2,1)} %bitcast.7, bf16[8,512,128]{2,1,0:T(8,128)(2,1)} %bitcast.8, f32[64,2048]{1,0:T(8,128)} %bitcast.9, f32[1,128]{1,0:T(1,128)} %bitcast.10), custom_call_target="tpu_custom_call" | custom-call | tf_op jit(solution)/shard_map/move_and_turn/pallas_call | solution.py:324
  26.7 1.3 %write_out.1 = (bf16[4096,128]{1,0:T(8,128)(2,1)}, bf16[8,512,128]{2,1,0:T(8,128)(2,1)}, f32[2,128]{1,0:T(2,128)}) custom-call(bf16[4096,128]{1,0:T(8,128)(2,1)S(1)} %get-tuple-element.9.refs_0_, bf16[8,512,128]{2,1,0:T(8,128)(2,1)S(1)} %get-tuple-element.10.refs_1_, f32[2,128]{1,0:T(2,128)S(1)} %get-tuple-element.11.refs_2_), custom_call_target="tpu_custom_call" | custom-call | tf_op jit(solution)/shard_map/write_out/pallas_call | solution.py:358

commit v8 on v7

--- a/solution.py
+++ b/solution.py
@@ -230,8 +230,8 @@
     pl.when(inner)(functools.partial(send_values, across))
     for offset in two_links:
         sends[1, offset].start()
+    send_values([pair for pair in pairs if pair not in across])
     pl.when(jnp.logical_not(inner))(functools.partial(send_values, across))
-    send_values([pair for pair in pairs if pair not in across])
     sends[1, (1, 0)].start()
 
     for copy in (local[0], local[1], local[3]):

time: 28.4 us -> 28.4 us (level)
  no operation moved by 1% of the time
where the time goes in v8:
time: 28.4 us; the launch traced here: 28.1 us
  Pallas kernels  27.4 us (96%)
  between operations  0.64 us (2%)
    pallas_call x1, Pallas kernels, shards(): pl.pallas_call(functools.partial(kernel, far, near, heads, offsets), out_...  26.1 us
    pallas_call x1, Pallas kernels, shards(): pl.pallas_call(write_out, out_shape=tuple((pltpu.HBM(r.shape, r.dtype) fo...  1.35 us

profile of v8, /device:TPU:0, one launch (start us, length us, event | category | flops | bytes accessed | tf_op | source)
XLA Modules:
  0.0 28.1 jit_solution(10587145029547605238)
XLA Ops:
  0.6 26.1 %move_and_turn.1 = (bf16[4096,128]{1,0:T(8,128)(2,1)S(1)}, bf16[8,512,128]{2,1,0:T(8,128)(2,1)S(1)}, f32[2,128]{1,0:T(2,128)S(1)}) custom-call(bf16[8,512,128]{2,1,0:T(8,128)(2,1)} %bitcast.7, bf16[8,512,128]{2,1,0:T(8,128)(2,1)} %bitcast.8, f32[64,2048]{1,0:T(8,128)} %bitcast.9, f32[1,128]{1,0:T(1,128)} %bitcast.10), custom_call_target="tpu_custom_call" | custom-call | tf_op jit(solution)/shard_map/move_and_turn/pallas_call | solution.py:324
  26.7 1.3 %write_out.1 = (bf16[4096,128]{1,0:T(8,128)(2,1)}, bf16[8,512,128]{2,1,0:T(8,128)(2,1)}, f32[2,128]{1,0:T(2,128)}) custom-call(bf16[4096,128]{1,0:T(8,128)(2,1)S(1)} %get-tuple-element.9.refs_0_, bf16[8,512,128]{2,1,0:T(8,128)(2,1)S(1)} %get-tuple-element.10.refs_1_, f32[2,128]{1,0:T(2,128)S(1)} %get-tuple-element.11.refs_2_), custom_call_target="tpu_custom_call" | custom-call | tf_op jit(solution)/shard_map/write_out/pallas_call | solution.py:358
